TPU v7x, 32 devices: a whole 2x2x4 slice. The times are simulated.
32 devices in a mesh: blk: 4 (over y, core), grp: 8 (over z, x).
Axes of the slice: x: 2, y: 2, z: 4, core: 2. Of those that a mesh axis runs over, the one named last changes fastest.
Arguments:
- gas_state: bfloat16 [16, 32, 32768], P(None, None, ('grp', 'blk')), may hold values from -6 to 6
- cos_zenith: bfloat16 [32768], P(('grp', 'blk')), may hold values from 0.049804688 to 1
- daylit: int32 [32768], P(('grp', 'blk')), may hold values from 0 to 1
- fine_area: float32 [131072], P(('grp', 'blk')), may hold values from 0.25 to 4
- fine_albedo: float32 [2, 131072], P(None, ('grp', 'blk')), may hold values from 0.05 to 0.85
- parent_of: int32 [131072], P(('grp', 'blk')), may hold values from 0 to 4095, as said below
- optics_weight: bfloat16 [64, 16], replicated, may hold values from -1.5 to 1.5
- solar_weight: float32 [32], replicated, may hold values from 0.01 to 0.1
- neighbours: int32 [3, 32768], P(None, ('grp', 'blk')), may hold values from 0 to 32767, as said below
- side_weight: float32 [3, 32768], P(None, ('grp', 'blk')), may hold values from 0.05 to 0.3
Outputs:
- fluxes: float32 [2, 33, 32768], P(None, None, ('grp', 'blk'))
Inputs may be any that keep to these rules, and one draw needn't show every extreme that they name: `parent_of`: the fine cells of one index of grp have their parents among that index's columns, numbered from 0 within it; each column has exactly 4 fine cells, and the 128 fine cells of an aligned block share 128 // 4 consecutive columns. `neighbours`: every neighbour lies within 128 columns of its column and among the columns of the same index of grp; a neighbour may be the column itself.
All inputs are finite; a program needn't handle non-finite values.
Results may differ from a plain program's by a relative error of at most 0.0003.
Values may be sent and summed in bfloat16 or wider, within the bound.
A program may use at most 64 MiB of HBM per device.

v0:
```python
import functools

import jax
import jax.numpy as jnp
from jax import lax
from jax.experimental import pallas as pl
from jax.experimental.pallas import tpu as pltpu
from jax.sharding import PartitionSpec as P

CB = 128
FB = 128
ASYM = 0.8
TAU_SCALE = 0.08
SSA_MAX = 0.98
CHUNK = 8
VMEM = pltpu.VMEM


def round_up(value, multiple):
    return -(-value // multiple) * multiple


def local_albedo(area_ref, albedo_ref, parent_ref, span):
    blocks = area_ref.shape[0]
    area = area_ref[...]
    rows = [
        jnp.concatenate([albedo_ref[s : s + 1, b * FB : (b + 1) * FB] for b in range(blocks)], axis=0)
        for s in range(2)
    ]
    weights = [area, area * rows[0], area * rows[1]]
    weights = [jnp.transpose(w) for w in weights]
    parent = jnp.transpose(parent_ref[...])
    inside = parent & (span - 1)
    sums = [[], [], []]
    for j in range(span):
        hit = inside == j
        for q in range(3):
            sums[q].append(jnp.sum(jnp.where(hit, weights[q], 0.0), axis=0, keepdims=True))
    totals = [jnp.concatenate(s, axis=0) for s in sums]
    first = (totals[1] / totals[0]).astype(jnp.bfloat16).astype(jnp.float32)
    second = (totals[2] / totals[0]).astype(jnp.bfloat16).astype(jnp.float32)
    number = (parent[0:1] // span).astype(jnp.float32)
    return first, second, number


def albedo_kernel(span, area_ref, albedo_ref, parent_ref, out_ref):
    blocks = area_ref.shape[0]
    first, second, number = local_albedo(area_ref, albedo_ref, parent_ref, span)
    out_ref[...] = jnp.zeros_like(out_ref)
    out_ref[0:span, 0:blocks] = first
    out_ref[0:span, blocks : 2 * blocks] = second
    out_ref[span : span + 1, 0:blocks] = number


def pick_albedo(pieces, start_span, span, blocks, ncb):
    per = CB // span
    table = jnp.concatenate(
        [jnp.concatenate([p[0:span, s * blocks : (s + 1) * blocks] for p in pieces], axis=1) for s in range(2)],
        axis=0,
    ).astype(jnp.bfloat16)
    number = jnp.concatenate([p[span : span + 1, 0:blocks] for p in pieces], axis=1).astype(jnp.int32)
    total = number.shape[1]
    row = lax.broadcasted_iota(jnp.int32, (ncb, total), 0) * per + start_span
    parts = []
    for m in range(per):
        chosen = (number == row + m).astype(jnp.float32).astype(jnp.bfloat16)
        parts.append(
            lax.dot_general(chosen, table, (((1,), (1,)), ((), ())), preferred_element_type=jnp.float32)
        )
    direct = jnp.concatenate([p[:, 0:span] for p in parts], axis=1)
    diffuse = jnp.concatenate([p[:, span : 2 * span] for p in parts], axis=1)
    return direct, diffuse


def expand_weight(weight_ref, big_ref):
    rows, feats = weight_ref.shape
    half = big_ref.shape[1] // feats
    wide = feats * half
    source = lax.broadcasted_iota(jnp.int32, (feats, wide), 0)
    column = lax.broadcasted_iota(jnp.int32, (feats, wide), 1)
    spread = (column // half == source).astype(jnp.float32).astype(jnp.bfloat16)
    repeated = jnp.dot(weight_ref[...], spread, preferred_element_type=jnp.float32)
    level = lax.broadcasted_iota(jnp.int32, (rows, wide), 1) % half
    for l in range(half):
        big_ref[l * rows : (l + 1) * rows, :] = jnp.where(level == l, repeated, 0.0).astype(jnp.bfloat16)


def layer(mix, gpoints, rate, back, carry):
    direct, big_b, big_q = carry
    x = mix[:gpoints]
    y = mix[gpoints:]
    soft = jnp.maximum(x, 0.0) + jnp.log(1.0 + jnp.exp(-jnp.abs(x)))
    share = jnp.exp(soft * rate)
    th = jnp.tanh(0.5 * y)
    h = 0.5 * SSA_MAX
    w = h + h * th
    up1 = 1.25 + 0.75 * ASYM
    g1 = 2.0 - up1 * w
    c2 = 0.75 * (1.0 - ASYM)
    g2 = c2 * w
    minus = 2.0 - (up1 + c2) * w
    plus = 2.0 - (up1 - c2) * w
    square = minus * plus
    k = square * lax.rsqrt(square)
    q = jnp.exp((k * soft) * (-TAU_SCALE))
    q2 = q * q
    kp = k + g1
    km = k - g1
    d = kp + km * q2
    dd = km + kp * q2
    r = g2 - g2 * q2
    t2 = (k + k) * q
    below = direct * share
    scattered = w * (direct - below)
    rising = scattered * back
    falling = scattered - rising
    z = 1.0 / (d - r * big_b)
    t = t2 * z
    s = (r * big_q + d * rising) * z
    new_b = (r + dd * big_b) * z
    new_q = t * (big_q + big_b * rising) + falling
    return t, s, (below, new_b, new_q)


def solve_block(cb, gas_ref, big_ref, cos_ref, lit_ref, solar, surface, state_ref, flux_ref, up_row):
    feats, lev = gas_ref.shape[0], gas_ref.shape[1]
    gpoints = solar.shape[0]
    rows = 2 * gpoints
    half = big_ref.shape[1] // feats
    cols = pl.ds(pl.multiple_of(cb * CB, CB), CB)
    mu = cos_ref[pl.ds(cb, 1), :]
    lit = lit_ref[pl.ds(cb, 1), :]
    rate = jnp.broadcast_to(-TAU_SCALE / mu, (gpoints, CB))
    back = jnp.broadcast_to(0.5 * (1.0 - ASYM * mu), (gpoints, CB))
    top = solar * mu
    zero = jnp.zeros((gpoints, CB), jnp.float32)
    carry = (top, zero, zero)

    for part in range(lev // half):
        inputs = gas_ref[:, part * half : (part + 1) * half, cols].reshape(feats * half, CB)

        def down(step, carry, part=part, inputs=inputs):
            at = pl.multiple_of(step * (CHUNK * rows), CHUNK * rows)
            mix = jnp.dot(
                big_ref[pl.ds(at, CHUNK * rows), :], inputs, preferred_element_type=jnp.float32
            )
            for i in range(CHUNK):
                level = part * half + step * CHUNK + i
                state_ref[2, level] = carry[1]
                state_ref[3, level] = carry[2] + carry[0]
                t, s, carry = layer(mix[i * rows : (i + 1) * rows], gpoints, rate, back, carry)
                state_ref[0, level] = t
                state_ref[1, level] = s
            return carry

        carry = lax.fori_loop(0, half // CHUNK, down, carry)

    direct, big_b, big_q = carry
    direct_albedo, diffuse_albedo = surface(cb)
    up = (diffuse_albedo * big_q + direct_albedo * direct) / (1.0 - diffuse_albedo * big_b)
    flux_ref[lev : lev + 1, cols] = jnp.sum(big_b * up + big_q + direct, axis=0, keepdims=True) * lit
    flux_ref[up_row + lev : up_row + lev + 1, cols] = jnp.sum(up, axis=0, keepdims=True) * lit

    def back_up(step, up):
        first = pl.multiple_of(lev - CHUNK - step * CHUNK, CHUNK)
        downs, ups = [None] * CHUNK, [None] * CHUNK
        for i in reversed(range(CHUNK)):
            up = state_ref[0, first + i] * up + state_ref[1, first + i]
            down = state_ref[2, first + i] * up + state_ref[3, first + i]
            downs[i] = jnp.sum(down, axis=0, keepdims=True)
            ups[i] = jnp.sum(up, axis=0, keepdims=True)
        flux_ref[pl.ds(first, CHUNK), cols] = jnp.concatenate(downs, axis=0) * lit
        flux_ref[pl.ds(up_row + first, CHUNK), cols] = jnp.concatenate(ups, axis=0) * lit
        return up

    lax.fori_loop(0, lev // CHUNK, back_up, up)


def solar_column(solar_ref):
    row = solar_ref[...]
    n = row.shape[1]
    diagonal = lax.broadcasted_iota(jnp.int32, (n, n), 0) == lax.broadcasted_iota(jnp.int32, (n, n), 1)
    return jnp.sum(jnp.where(diagonal, row, 0.0), axis=1, keepdims=True)


def flux_kernel(
    n, span, blocks, gas_ref, cos_ref, lit_ref, weight_ref, solar_ref, pieces_ref,
    flux_ref, big_ref, state_ref, albedo_ref, cosf_ref, litf_ref,
):
    ncb = cos_ref.shape[0]
    lev = gas_ref.shape[1]
    start_span = lax.axis_index("blk") * (ncb * CB // span)
    expand_weight(weight_ref, big_ref)
    cosf_ref[...] = cos_ref[...].astype(jnp.float32)
    litf_ref[...] = lit_ref[...].astype(jnp.float32)
    direct, diffuse = pick_albedo([pieces_ref[i] for i in range(n)], start_span, span, blocks, ncb)
    albedo_ref[0] = direct
    albedo_ref[1] = diffuse
    solar = solar_column(solar_ref)
    flux_ref[...] = jnp.zeros_like(flux_ref)

    def surface(cb):
        return albedo_ref[0, pl.ds(cb, 1), :], albedo_ref[1, pl.ds(cb, 1), :]

    def one(cb, unused):
        solve_block(
            cb, gas_ref, big_ref, cosf_ref, litf_ref, solar, surface, state_ref, flux_ref,
            round_up(lev + 1, 8),
        )
        return unused

    lax.fori_loop(0, ncb, one, 0)


def side_block(window, centre, picked, weights):
    rows = window.shape[0]
    high = window.astype(jnp.bfloat16)
    low = (window - high.astype(jnp.float32)).astype(jnp.bfloat16)
    both = jnp.concatenate([high, low], axis=0)
    place = lax.broadcasted_iota(jnp.int32, (window.shape[1], CB), 0)
    result = centre
    for k in range(3):
        chosen = (place == picked[k : k + 1]).astype(jnp.float32).astype(jnp.bfloat16)
        beside = jnp.dot(both, chosen, preferred_element_type=jnp.float32)
        result = result + weights[k : k + 1] * (beside[:rows] + beside[rows:] - centre)
    return result


def side_kernel(flux_ref, low_ref, high_ref, neighbours_ref, weights_ref, out_ref, padded_ref):
    cols = flux_ref.shape[1]
    ncb = cols // CB
    interfaces = out_ref.shape[1]
    up_row = round_up(interfaces, 8)
    start = (lax.axis_index("grp") * lax.axis_size("blk") + lax.axis_index("blk")) * cols
    padded_ref[:, 0:CB] = low_ref[...]
    padded_ref[:, CB : CB + cols] = flux_ref[...]
    padded_ref[:, CB + cols :] = high_ref[...]
    for cb in range(ncb):
        own = slice(cb * CB, (cb + 1) * CB)
        picked = neighbours_ref[:, own] - (start + (cb - 1) * CB)
        result = side_block(
            padded_ref[:, cb * CB : (cb + 3) * CB],
            padded_ref[:, (cb + 1) * CB : (cb + 2) * CB],
            picked,
            weights_ref[:, own],
        )
        out_ref[0, :, own] = result[:interfaces]
        out_ref[1, :, own] = result[up_row : up_row + interfaces]


def local(
    gas_state, cos_zenith, daylit, fine_area, fine_albedo, parent_of,
    optics_weight, solar_weight, neighbours, side_weight,
):
    n = lax.axis_size("blk")
    feats, lev, cols = gas_state.shape
    gpoints = solar_weight.shape[0]
    ncb = cols // CB
    blocks = fine_area.shape[0] // FB
    span = cols // blocks
    up_row = round_up(lev + 1, 8)
    half = 16
    full = pl.BlockSpec(memory_space=VMEM)
    pieces = pl.pallas_call(
        functools.partial(albedo_kernel, span),
        out_shape=jax.ShapeDtypeStruct((span + 8, 128), jnp.float32),
        in_specs=[full] * 3,
        out_specs=full,
    )(fine_area.reshape(blocks, FB), fine_albedo, parent_of.reshape(blocks, FB))
    pieces = lax.all_gather(pieces, "blk")
    flux = pl.pallas_call(
        functools.partial(flux_kernel, n, span, blocks),
        out_shape=jax.ShapeDtypeStruct((2 * up_row, cols), jnp.float32),
        in_specs=[full] * 6,
        out_specs=full,
        scratch_shapes=[
            VMEM((half * 2 * gpoints, half * feats), jnp.bfloat16),
            VMEM((4, lev, gpoints, CB), jnp.float32),
            VMEM((2, ncb, CB), jnp.float32),
            VMEM((ncb, CB), jnp.float32),
            VMEM((ncb, CB), jnp.float32),
        ],
    )(
        gas_state, cos_zenith.reshape(ncb, CB), daylit.reshape(ncb, CB), optics_weight,
        solar_weight.reshape(1, gpoints), pieces,
    )
    forward = [(i, i + 1) for i in range(n - 1)]
    backward = [(i + 1, i) for i in range(n - 1)]
    low = lax.ppermute(flux[:, cols - CB :], "blk", forward)
    high = lax.ppermute(flux[:, :CB], "blk", backward)
    return pl.pallas_call(
        side_kernel,
        out_shape=jax.ShapeDtypeStruct((2, lev + 1, cols), jnp.float32),
        in_specs=[full] * 5,
        out_specs=full,
        scratch_shapes=[VMEM((2 * up_row, cols + 2 * CB), jnp.float32)],
    )(flux, low, high, neighbours, side_weight)


def solution(mesh):
    columns = P(("grp", "blk"))
    last = P(None, ("grp", "blk"))
    in_specs = (
        P(None, None, ("grp", "blk")), columns, columns, columns, last, columns, P(), P(), last, last,
    )
    out_specs = P(None, None, ("grp", "blk"))
    return jax.shard_map(local, mesh=mesh, in_specs=in_specs, out_specs=out_specs, check_vma=False)
```

profile of v0, /device:TPU:1, one launch (start us, length us, event | category | flops | bytes accessed | tf_op | source)
XLA Modules:
  0.0 43.3 jit_solution(3303562596984901334)
XLA Ops:
  0.0 1.4 %copy.11.weight_ref = bf16[64,16]{1,0:T(8,128)(2,1)} copy(bf16[64,16]{0,1:T(8,128)(2,1)} %param.16) | data formatting | bytes 4096 | tf_op args[6]
  1.4 2.3 %shard_map.100 = f32[40,128]{1,0:T(8,128)} custom-call(f32[32,128]{1,0:T(8,128)} %bitcast.7, f32[2,4096]{1,0:T(2,128)} %albedo_ref.1, s32[32,128]{1,0:T(8,128)} %bitcast.8), custom_call_target="tpu_custom_call" | custom-call | tf_op jit(solution)/shard_map/pallas_call | solution.py:264
  3.6 8.1 %all-gather = f32[160,128]{1,0:T(8,128)} all-gather(f32[40,128]{1,0:T(8,128)} %shard_map.100), channel_id=2, replica_groups=mesh['blk'=4,'grp'=8] {'blk'}, dimensions={0}, use_global_device_ids=true | all-gather | bytes 102400 | tf_op jit(solution)/shard_map/all_gather | solution.py:270
  11.7 18.9 %shard_map.101.flux_ref = f32[80,1024]{1,0:T(8,128)} custom-call(bf16[16,32,1024]{2,1,0:T(8,128)(2,1)} %gas_ref.1, bf16[8,128]{1,0:T(8,128)(2,1)} %bitcast.10, s32[8,128]{1,0:T(8,128)} %bitcast.9, bf16[64,16]{1,0:T(8,128)(2,1)} %copy.11.weight_ref, f32[1,32]{1,0:T(1,128)} %bitcast.11, f32[4,40,128]{2,1,0:T(8,128)} %bitcast.6), custom_call_target="tpu_custom_call" | custom-call | tf_op jit(solution)/shard_map/pallas_call | solution.py:271
  30.6 0.8 %fusion = (f32[80,128]{1,0:T(8,128)S(1)}, f32[80,128]{1,0:T(8,128)S(1)}) fusion(f32[80,1024]{1,0:T(8,128)} %shard_map.101.flux_ref), kind=kLoop, calls=%fused_computation | loop fusion | bytes 163840 | tf_op jit(solution)/shard_map/slice | solution.py:290
  31.4 2.1 %collective-permute-start.1 = (f32[80,128]{1,0:T(8,128)S(1)}, f32[80,128]{1,0:T(8,128)S(1)}, u32[]{:S(2)}, u32[]{:S(2)}) collective-permute-start(f32[80,128]{1,0:T(8,128)S(1)} %get-tuple-element.5), channel_id=1, source_target_pairs={{8,0},{16,8},{24,16},{9,1},{17,9},{25,17},{10,2},{18,10},{26,18},{... | collective-permute-start | bytes 122888 | tf_op jit(solution)/shard_map/ppermute | solution.py:290
  33.5 3.5 %collective-permute-start = (f32[80,128]{1,0:T(8,128)S(1)}, f32[80,128]{1,0:T(8,128)S(1)}, u32[]{:S(2)}, u32[]{:S(2)}) collective-permute-start(f32[80,128]{1,0:T(8,128)S(1)} %get-tuple-element.6), channel_id=1, source_target_pairs={{0,8},{8,16},{16,24},{1,9},{9,17},{17,25},{2,10},{10,18},{18,26},{... | collective-permute-start | bytes 122888 | tf_op jit(solution)/shard_map/ppermute | solution.py:289
  37.0 0.0 collective-permute-done.1.high_ref
  37.0 0.0 copy-start
  37.0 1.1 %collective-permute-done.low_ref = f32[80,128]{1,0:T(8,128)S(1)} collective-permute-done((f32[80,128]{1,0:T(8,128)S(1)}, f32[80,128]{1,0:T(8,128)S(1)}, u32[]{:S(2)}, u32[]{:S(2)}) %collective-permute-start) | collective-permute-done | bytes 40992 | tf_op jit(solution)/shard_map/ppermute | solution.py:289
  38.1 0.0 copy-done
  38.1 0.0 copy-start.1
  38.1 0.6 %copy-done.1 = f32[80,128]{1,0:T(8,128)} copy-done((f32[80,128]{1,0:T(8,128)}, f32[80,128]{1,0:T(8,128)S(1)}, u32[]{:S(2)}) %copy-start.1) | copy-done | bytes 40984
  38.7 2.7 %shard_map.102 = f32[2,33,1024]{2,1,0:T(8,128)} custom-call(f32[80,1024]{1,0:T(8,128)} %shard_map.101.flux_ref, f32[80,128]{1,0:T(8,128)} %copy-done.1, f32[80,128]{1,0:T(8,128)} %copy-done, s32[3,1024]{1,0:T(4,128)} %neighbours_ref.1, f32[3,1024]{1,0:T(4,128)} %weights_ref.1), custom_call_target="tpu_custom_call" | custom-call | tf_op jit(solution)/shard_map/pallas_call | solution.py:291
  41.4 1.9 %copy.12 = f32[2,33,1024]{2,0,1:T(2,128)} copy(f32[2,33,1024]{2,1,0:T(8,128)} %shard_map.102) | data formatting | bytes 540672 | tf_op jit(solution)/shard_map/pallas_call | solution.py:291
Async XLA Ops:
  31.4 5.6 %collective-permute-start.1 = (f32[80,128]{1,0:T(8,128)S(1)}, f32[80,128]{1,0:T(8,128)S(1)}, u32[]{:S(2)}, u32[]{:S(2)}) collective-permute-start(f32[80,128]{1,0:T(8,128)S(1)} %get-tuple-element.5), channel_id=1, source_target_pairs={{8,0},{16,8},{24,16},{9,1},{17,9},{25,17},{10,2},{18,10},{26,18},{... | collective-permute-start | bytes 122888 | tf_op jit(solution)/shard_map/ppermute | solution.py:290
  33.5 4.5 %collective-permute-start = (f32[80,128]{1,0:T(8,128)S(1)}, f32[80,128]{1,0:T(8,128)S(1)}, u32[]{:S(2)}, u32[]{:S(2)}) collective-permute-start(f32[80,128]{1,0:T(8,128)S(1)} %get-tuple-element.6), channel_id=1, source_target_pairs={{0,8},{8,16},{16,24},{1,9},{9,17},{17,25},{2,10},{10,18},{18,26},{... | collective-permute-start | bytes 122888 | tf_op jit(solution)/shard_map/ppermute | solution.py:289
  37.0 1.1 %copy-start = (f32[80,128]{1,0:T(8,128)}, f32[80,128]{1,0:T(8,128)S(1)}, u32[]{:S(2)}) copy-start(f32[80,128]{1,0:T(8,128)S(1)} %collective-permute-done.1.high_ref) | copy-start | bytes 122884
  38.1 0.6 %copy-start.1 = (f32[80,128]{1,0:T(8,128)}, f32[80,128]{1,0:T(8,128)S(1)}, u32[]{:S(2)}) copy-start(f32[80,128]{1,0:T(8,128)S(1)} %collective-permute-done.low_ref) | copy-start | bytes 122884
where the time goes:
time: 43.7 us; the launch traced here: 43.3 us
  Pallas kernels  23.9 us (55%)
  blocking collectives  8.08 us (18%)
  starting transfers between devices  5.55 us (13%)
  local copies, waits for them, and re-layouts  4.68 us (11%)
  waiting for transfers between devices  1.06 us (2%)
    pallas_call x1, Pallas kernels, local(): pl.pallas_call(functools.partial(flux_kernel, n, span, blocks), out_shape...  18.9 us
    all_gather x1, blocking collectives, local(): pieces = lax.all_gather(pieces, 'blk')  8.08 us
    ppermute x1, starting transfers between devices, local(): low = lax.ppermute(flux[:, cols - CB:], 'blk', forward)  3.46 us
    pallas_call x1, Pallas kernels, local(): pl.pallas_call(side_kernel, out_shape=jax.ShapeDtypeStruct((2, lev + 1, c...  2.7 us
    pallas_call x1, Pallas kernels, local(): pl.pallas_call(functools.partial(albedo_kernel, span), out_shape=jax.Shap...  2.28 us
    ppermute x1, starting transfers between devices, local(): high = lax.ppermute(flux[:, :CB], 'blk', backward)  2.09 us
    unnamed x5, local copies, waits for them, and re-layouts  1.99 us
    pallas_call x1, local copies, waits for them, and re-layouts, local(): pl.pallas_call(side_kernel, out_shape=jax.ShapeDtypeStruct((2, lev + 1, c...  1.89 us
  transfers between devices with their start and end apart: 2, of which 1 were waited for; matrix products, arithmetic and copies ran while one was open for 0% of the time, Pallas kernels for 0%

commit v1 on v0

--- a/solution.py
+++ b/solution.py
@@ -43,15 +43,6 @@
     return first, second, number
 
 
-def albedo_kernel(span, area_ref, albedo_ref, parent_ref, out_ref):
-    blocks = area_ref.shape[0]
-    first, second, number = local_albedo(area_ref, albedo_ref, parent_ref, span)
-    out_ref[...] = jnp.zeros_like(out_ref)
-    out_ref[0:span, 0:blocks] = first
-    out_ref[0:span, blocks : 2 * blocks] = second
-    out_ref[span : span + 1, 0:blocks] = number
-
-
 def pick_albedo(pieces, start_span, span, blocks, ncb):
     per = CB // span
     table = jnp.concatenate(
@@ -73,13 +64,15 @@
 
 
 def expand_weight(weight_ref, big_ref):
-    rows, feats = weight_ref.shape
+    feats, rows = weight_ref.shape
     half = big_ref.shape[1] // feats
     wide = feats * half
     source = lax.broadcasted_iota(jnp.int32, (feats, wide), 0)
     column = lax.broadcasted_iota(jnp.int32, (feats, wide), 1)
     spread = (column // half == source).astype(jnp.float32).astype(jnp.bfloat16)
-    repeated = jnp.dot(weight_ref[...], spread, preferred_element_type=jnp.float32)
+    repeated = lax.dot_general(
+        weight_ref[...], spread, (((0,), (0,)), ((), ())), preferred_element_type=jnp.float32
+    )
     level = lax.broadcasted_iota(jnp.int32, (rows, wide), 1) % half
     for l in range(half):
         big_ref[l * rows : (l + 1) * rows, :] = jnp.where(level == l, repeated, 0.0).astype(jnp.bfloat16)
@@ -122,14 +115,13 @@
     return t, s, (below, new_b, new_q)
 
 
-def solve_block(cb, gas_ref, big_ref, cos_ref, lit_ref, solar, surface, state_ref, flux_ref, up_row):
+def descend(cb, gas_ref, big_ref, cos_ref, solar, state_ref, end_ref):
     feats, lev = gas_ref.shape[0], gas_ref.shape[1]
     gpoints = solar.shape[0]
     rows = 2 * gpoints
     half = big_ref.shape[1] // feats
     cols = pl.ds(pl.multiple_of(cb * CB, CB), CB)
     mu = cos_ref[pl.ds(cb, 1), :]
-    lit = lit_ref[pl.ds(cb, 1), :]
     rate = jnp.broadcast_to(-TAU_SCALE / mu, (gpoints, CB))
     back = jnp.broadcast_to(0.5 * (1.0 - ASYM * mu), (gpoints, CB))
     top = solar * mu
@@ -154,23 +146,33 @@
             return carry
 
         carry = lax.fori_loop(0, half // CHUNK, down, carry)
-
-    direct, big_b, big_q = carry
-    direct_albedo, diffuse_albedo = surface(cb)
+    for i in range(3):
+        end_ref[i] = carry[i]
+
+
+def ascend(cb, albedo_ref, lit_ref, state_ref, end_ref, flux_ref):
+    lev = state_ref.shape[1]
+    lit = lit_ref[pl.ds(cb, 1), :]
+    direct, big_b, big_q = end_ref[0], end_ref[1], end_ref[2]
+    direct_albedo = albedo_ref[0, pl.ds(cb, 1), :]
+    diffuse_albedo = albedo_ref[1, pl.ds(cb, 1), :]
     up = (diffuse_albedo * big_q + direct_albedo * direct) / (1.0 - diffuse_albedo * big_b)
-    flux_ref[lev : lev + 1, cols] = jnp.sum(big_b * up + big_q + direct, axis=0, keepdims=True) * lit
-    flux_ref[up_row + lev : up_row + lev + 1, cols] = jnp.sum(up, axis=0, keepdims=True) * lit
+    last = [
+        jnp.sum(big_b * up + big_q + direct, axis=0, keepdims=True) * lit,
+        jnp.sum(up, axis=0, keepdims=True) * lit,
+        jnp.zeros((flux_ref.shape[0] - 2 * lev - 2, CB), jnp.float32),
+    ]
+    flux_ref[2 * lev :, :] = jnp.concatenate(last, axis=0)
 
     def back_up(step, up):
         first = pl.multiple_of(lev - CHUNK - step * CHUNK, CHUNK)
-        downs, ups = [None] * CHUNK, [None] * CHUNK
+        sums = [None] * (2 * CHUNK)
         for i in reversed(range(CHUNK)):
             up = state_ref[0, first + i] * up + state_ref[1, first + i]
             down = state_ref[2, first + i] * up + state_ref[3, first + i]
-            downs[i] = jnp.sum(down, axis=0, keepdims=True)
-            ups[i] = jnp.sum(up, axis=0, keepdims=True)
-        flux_ref[pl.ds(first, CHUNK), cols] = jnp.concatenate(downs, axis=0) * lit
-        flux_ref[pl.ds(up_row + first, CHUNK), cols] = jnp.concatenate(ups, axis=0) * lit
+            sums[2 * i] = jnp.sum(down, axis=0, keepdims=True)
+            sums[2 * i + 1] = jnp.sum(up, axis=0, keepdims=True)
+        flux_ref[pl.ds(pl.multiple_of(2 * first, 2 * CHUNK), 2 * CHUNK), :] = jnp.concatenate(sums, axis=0) * lit
         return up
 
     lax.fori_loop(0, lev // CHUNK, back_up, up)
@@ -184,32 +186,88 @@
 
 
 def flux_kernel(
-    n, span, blocks, gas_ref, cos_ref, lit_ref, weight_ref, solar_ref, pieces_ref,
-    flux_ref, big_ref, state_ref, albedo_ref, cosf_ref, litf_ref,
+    n, span, gas_ref, cos_ref, lit_ref, weight_ref, solar_ref, area_ref, fine_albedo_ref, parent_ref,
+    flux_ref, big_ref, state_ref, end_ref, albedo_ref, cosf_ref, litf_ref, mine_ref, pieces_ref,
+    edge_ref, halo_ref, send_sem, recv_sem, edge_send, edge_recv,
 ):
     ncb = cos_ref.shape[0]
-    lev = gas_ref.shape[1]
-    start_span = lax.axis_index("blk") * (ncb * CB // span)
+    blocks = area_ref.shape[0]
+    me = lax.axis_index("blk")
+    peers = [lax.rem(me + shift, n) for shift in range(1, n)]
+    mesh_id = pl.DeviceIdType.MESH
+
+    barrier = pltpu.get_barrier_semaphore()
+    for peer in peers:
+        pl.semaphore_signal(barrier, inc=1, device_id={"blk": peer}, device_id_type=mesh_id)
+
+    first, second, number = local_albedo(area_ref, fine_albedo_ref, parent_ref, span)
+    mine_ref[...] = jnp.zeros_like(mine_ref)
+    mine_ref[0:span, 0:blocks] = first
+    mine_ref[0:span, blocks : 2 * blocks] = second
+    mine_ref[span : span + 1, 0:blocks] = number
     expand_weight(weight_ref, big_ref)
     cosf_ref[...] = cos_ref[...].astype(jnp.float32)
     litf_ref[...] = lit_ref[...].astype(jnp.float32)
-    direct, diffuse = pick_albedo([pieces_ref[i] for i in range(n)], start_span, span, blocks, ncb)
+    solar = solar_column(solar_ref)
+
+    pl.semaphore_wait(barrier, n - 1)
+    sends = []
+    for i, peer in enumerate(peers):
+        copy = pltpu.make_async_remote_copy(
+            src_ref=mine_ref,
+            dst_ref=pieces_ref.at[i],
+            send_sem=send_sem.at[i],
+            recv_sem=recv_sem.at[i],
+            device_id={"blk": peer},
+            device_id_type=mesh_id,
+        )
+        copy.start()
+        sends.append(copy)
+
+    def edge_down(i, unused):
+        descend(i * (ncb - 1), gas_ref, big_ref, cosf_ref, solar, state_ref.at[i], end_ref.at[i])
+        return unused
+
+    lax.fori_loop(0, 2, edge_down, 0)
+    for copy in sends:
+        copy.wait()
+    start_span = me * (ncb * CB // span)
+    pieces = [mine_ref[...]] + [pieces_ref[i] for i in range(n - 1)]
+    direct, diffuse = pick_albedo(pieces, start_span, span, blocks, ncb)
     albedo_ref[0] = direct
     albedo_ref[1] = diffuse
-    solar = solar_column(solar_ref)
-    flux_ref[...] = jnp.zeros_like(flux_ref)
-
-    def surface(cb):
-        return albedo_ref[0, pl.ds(cb, 1), :], albedo_ref[1, pl.ds(cb, 1), :]
+
+    def edge_up(i, unused):
+        ascend(i * (ncb - 1), albedo_ref, litf_ref, state_ref.at[i], end_ref.at[i], edge_ref.at[i])
+        return unused
+
+    lax.fori_loop(0, 2, edge_up, 0)
+    sends = []
+    for i, peer in ((0, peers[-1]), (1, peers[0])):
+        copy = pltpu.make_async_remote_copy(
+            src_ref=edge_ref.at[i],
+            dst_ref=halo_ref.at[i],
+            send_sem=edge_send.at[i],
+            recv_sem=edge_recv.at[i],
+            device_id={"blk": peer},
+            device_id_type=mesh_id,
+        )
+        copy.start()
+        sends.append(copy)
+    flux_ref[:, CB : 2 * CB] = edge_ref[0]
+    flux_ref[:, ncb * CB : (ncb + 1) * CB] = edge_ref[1]
 
     def one(cb, unused):
-        solve_block(
-            cb, gas_ref, big_ref, cosf_ref, litf_ref, solar, surface, state_ref, flux_ref,
-            round_up(lev + 1, 8),
-        )
+        own = pl.ds(pl.multiple_of((cb + 1) * CB, CB), CB)
+        descend(cb, gas_ref, big_ref, cosf_ref, solar, state_ref.at[0], end_ref.at[0])
+        ascend(cb, albedo_ref, litf_ref, state_ref.at[0], end_ref.at[0], flux_ref.at[:, own])
         return unused
 
-    lax.fori_loop(0, ncb, one, 0)
+    lax.fori_loop(1, ncb - 1, one, 0)
+    for copy in sends:
+        copy.wait()
+    flux_ref[:, 0:CB] = halo_ref[1]
+    flux_ref[:, (ncb + 1) * CB :] = halo_ref[0]
 
 
 def side_block(window, centre, picked, weights):
@@ -226,15 +284,10 @@
     return result
 
 
-def side_kernel(flux_ref, low_ref, high_ref, neighbours_ref, weights_ref, out_ref, padded_ref):
-    cols = flux_ref.shape[1]
+def side_kernel(padded_ref, neighbours_ref, weights_ref, out_ref):
+    interfaces, parts, cols = out_ref.shape
     ncb = cols // CB
-    interfaces = out_ref.shape[1]
-    up_row = round_up(interfaces, 8)
     start = (lax.axis_index("grp") * lax.axis_size("blk") + lax.axis_index("blk")) * cols
-    padded_ref[:, 0:CB] = low_ref[...]
-    padded_ref[:, CB : CB + cols] = flux_ref[...]
-    padded_ref[:, CB + cols :] = high_ref[...]
     for cb in range(ncb):
         own = slice(cb * CB, (cb + 1) * CB)
         picked = neighbours_ref[:, own] - (start + (cb - 1) * CB)
@@ -244,8 +297,7 @@
             picked,
             weights_ref[:, own],
         )
-        out_ref[0, :, own] = result[:interfaces]
-        out_ref[1, :, own] = result[up_row : up_row + interfaces]
+        out_ref[:, :, own] = result[: parts * interfaces].reshape(interfaces, parts, CB)
 
 
 def local(
@@ -258,43 +310,43 @@
     ncb = cols // CB
     blocks = fine_area.shape[0] // FB
     span = cols // blocks
-    up_row = round_up(lev + 1, 8)
+    rows = round_up(2 * (lev + 1), 8)
     half = 16
     full = pl.BlockSpec(memory_space=VMEM)
-    pieces = pl.pallas_call(
-        functools.partial(albedo_kernel, span),
-        out_shape=jax.ShapeDtypeStruct((span + 8, 128), jnp.float32),
-        in_specs=[full] * 3,
-        out_specs=full,
-    )(fine_area.reshape(blocks, FB), fine_albedo, parent_of.reshape(blocks, FB))
-    pieces = lax.all_gather(pieces, "blk")
-    flux = pl.pallas_call(
-        functools.partial(flux_kernel, n, span, blocks),
-        out_shape=jax.ShapeDtypeStruct((2 * up_row, cols), jnp.float32),
-        in_specs=[full] * 6,
+    padded = pl.pallas_call(
+        functools.partial(flux_kernel, n, span),
+        out_shape=jax.ShapeDtypeStruct((rows, cols + 2 * CB), jnp.float32),
+        in_specs=[full] * 8,
         out_specs=full,
         scratch_shapes=[
             VMEM((half * 2 * gpoints, half * feats), jnp.bfloat16),
-            VMEM((4, lev, gpoints, CB), jnp.float32),
+            VMEM((2, 4, lev, gpoints, CB), jnp.float32),
+            VMEM((2, 3, gpoints, CB), jnp.float32),
             VMEM((2, ncb, CB), jnp.float32),
             VMEM((ncb, CB), jnp.float32),
             VMEM((ncb, CB), jnp.float32),
+            VMEM((span + 8, 128), jnp.float32),
+            VMEM((n - 1, span + 8, 128), jnp.float32),
+            VMEM((2, rows, CB), jnp.float32),
+            VMEM((2, rows, CB), jnp.float32),
+            pltpu.SemaphoreType.DMA((n - 1,)),
+            pltpu.SemaphoreType.DMA((n - 1,)),
+            pltpu.SemaphoreType.DMA((2,)),
+            pltpu.SemaphoreType.DMA((2,)),
         ],
+        compiler_params=pltpu.CompilerParams(collective_id=0, has_side_effects=True),
     )(
-        gas_state, cos_zenith.reshape(ncb, CB), daylit.reshape(ncb, CB), optics_weight,
-        solar_weight.reshape(1, gpoints), pieces,
+        gas_state, cos_zenith.reshape(ncb, CB), daylit.reshape(ncb, CB), optics_weight.T,
+        solar_weight.reshape(1, gpoints), fine_area.reshape(blocks, FB), fine_albedo,
+        parent_of.reshape(blocks, FB),
     )
-    forward = [(i, i + 1) for i in range(n - 1)]
-    backward = [(i + 1, i) for i in range(n - 1)]
-    low = lax.ppermute(flux[:, cols - CB :], "blk", forward)
-    high = lax.ppermute(flux[:, :CB], "blk", backward)
-    return pl.pallas_call(
+    result = pl.pallas_call(
         side_kernel,
-        out_shape=jax.ShapeDtypeStruct((2, lev + 1, cols), jnp.float32),
-        in_specs=[full] * 5,
+        out_shape=jax.ShapeDtypeStruct((lev + 1, 2, cols), jnp.float32),
+        in_specs=[full] * 3,
         out_specs=full,
-        scratch_shapes=[VMEM((2 * up_row, cols + 2 * CB), jnp.float32)],
-    )(flux, low, high, neighbours, side_weight)
+    )(padded, neighbours, side_weight)
+    return jnp.transpose(result, (1, 0, 2))
 
 
 def solution(mesh):

time: 43.7 us -> 25.2 us (0.58)
  the two profiles are of different devices: /device:TPU:1 before, /device:TPU:0 now
where the time goes in v1:
time: 25.2 us; the launch traced here: 25.1 us
  Pallas kernels  25.1 us (100%)
    pallas_call x1, Pallas kernels, local(): pl.pallas_call(functools.partial(flux_kernel, n, span), out_shape=jax.Sha...  22.3 us
    pallas_call x1, Pallas kernels, local(): pl.pallas_call(side_kernel, out_shape=jax.ShapeDtypeStruct((lev + 1, 2, c...  2.82 us

profile of v1, /device:TPU:0, one launch (start us, length us, event | category | flops | bytes accessed | tf_op | source)
XLA Modules:
  0.0 25.1 jit_solution(11753602977427978130)
XLA Ops:
  0.0 22.3 %shard_map.100.padded_ref = f32[72,1280]{1,0:T(8,128)} custom-call(bf16[16,32,1024]{2,1,0:T(8,128)(2,1)} %gas_ref.1, bf16[8,128]{1,0:T(8,128)(2,1)} %bitcast.11, s32[8,128]{1,0:T(8,128)} %bitcast.9, bf16[16,64]{1,0:T(8,128)(2,1)} %bitcast.10, f32[1,32]{1,0:T(1,128)} %bitcast.12, f32[32,128]{1,0:T(8,128)} %bitcast.7, f32[2,4096]{1,0:T(2,128)} %fine_albedo_ref.1, ...), custom_call_target="tpu_custom_call" | custom-call | tf_op jit(solution)/shard_map/pallas_call | solution.py:316
  22.3 2.8 %shard_map.101 = f32[33,2,1024]{2,1,0:T(2,128)} custom-call(f32[72,1280]{1,0:T(8,128)} %shard_map.100.padded_ref, s32[3,1024]{1,0:T(4,128)} %neighbours_ref.1, f32[3,1024]{1,0:T(4,128)} %weights_ref.1), custom_call_target="tpu_custom_call" | custom-call | tf_op jit(solution)/shard_map/pallas_call | solution.py:343

commit v2 on v1

--- a/solution.py
+++ b/solution.py
@@ -1,4 +1,5 @@
 import functools
+import math
 
 import jax
 import jax.numpy as jnp
@@ -12,6 +13,7 @@
 ASYM = 0.8
 TAU_SCALE = 0.08
 SSA_MAX = 0.98
+LOG2E = math.log2(math.e)
 CHUNK = 8
 VMEM = pltpu.VMEM
 
@@ -27,19 +29,16 @@
         jnp.concatenate([albedo_ref[s : s + 1, b * FB : (b + 1) * FB] for b in range(blocks)], axis=0)
         for s in range(2)
     ]
-    weights = [area, area * rows[0], area * rows[1]]
-    weights = [jnp.transpose(w) for w in weights]
-    parent = jnp.transpose(parent_ref[...])
+    weights = jnp.transpose(jnp.concatenate([area, area * rows[0], area * rows[1]], axis=0))
+    parent = jnp.transpose(jnp.concatenate([parent_ref[...]] * 3, axis=0))
     inside = parent & (span - 1)
-    sums = [[], [], []]
-    for j in range(span):
-        hit = inside == j
-        for q in range(3):
-            sums[q].append(jnp.sum(jnp.where(hit, weights[q], 0.0), axis=0, keepdims=True))
-    totals = [jnp.concatenate(s, axis=0) for s in sums]
-    first = (totals[1] / totals[0]).astype(jnp.bfloat16).astype(jnp.float32)
-    second = (totals[2] / totals[0]).astype(jnp.bfloat16).astype(jnp.float32)
-    number = (parent[0:1] // span).astype(jnp.float32)
+    totals = jnp.concatenate(
+        [jnp.sum(jnp.where(inside == j, weights, 0.0), axis=0, keepdims=True) for j in range(span)], axis=0
+    )
+    share = totals[:, :blocks]
+    first = (totals[:, blocks : 2 * blocks] / share).astype(jnp.bfloat16).astype(jnp.float32)
+    second = (totals[:, 2 * blocks :] / share).astype(jnp.bfloat16).astype(jnp.float32)
+    number = (parent[0:1, :blocks] // span).astype(jnp.float32)
     return first, second, number
 
 
@@ -73,6 +72,8 @@
     repeated = lax.dot_general(
         weight_ref[...], spread, (((0,), (0,)), ((), ())), preferred_element_type=jnp.float32
     )
+    row = lax.broadcasted_iota(jnp.int32, (rows, wide), 0)
+    repeated = jnp.where(row < rows // 2, repeated, 0.5 * repeated)
     level = lax.broadcasted_iota(jnp.int32, (rows, wide), 1) % half
     for l in range(half):
         big_ref[l * rows : (l + 1) * rows, :] = jnp.where(level == l, repeated, 0.0).astype(jnp.bfloat16)
@@ -81,21 +82,16 @@
 def layer(mix, gpoints, rate, back, carry):
     direct, big_b, big_q = carry
     x = mix[:gpoints]
-    y = mix[gpoints:]
-    soft = jnp.maximum(x, 0.0) + jnp.log(1.0 + jnp.exp(-jnp.abs(x)))
-    share = jnp.exp(soft * rate)
-    th = jnp.tanh(0.5 * y)
-    h = 0.5 * SSA_MAX
-    w = h + h * th
-    up1 = 1.25 + 0.75 * ASYM
-    g1 = 2.0 - up1 * w
-    c2 = 0.75 * (1.0 - ASYM)
-    g2 = c2 * w
-    minus = 2.0 - (up1 + c2) * w
-    plus = 2.0 - (up1 - c2) * w
-    square = minus * plus
+    soft = jnp.maximum(x, 0.0) + jnp.log(1.0 + jnp.exp2(jnp.abs(x) * (-LOG2E)))
+    below = direct * jnp.exp2(soft * rate)
+    swing = (0.5 * SSA_MAX) * jnp.tanh(mix[gpoints:])
+    w = swing + 0.5 * SSA_MAX
+    absorbed = (1.0 - 0.5 * SSA_MAX) - swing
+    g2 = (0.375 * (1.0 - ASYM)) * w
+    g1 = absorbed + g2
+    square = absorbed * (g1 + g2)
     k = square * lax.rsqrt(square)
-    q = jnp.exp((k * soft) * (-TAU_SCALE))
+    q = jnp.exp2((k * soft) * (-2.0 * TAU_SCALE * LOG2E))
     q2 = q * q
     kp = k + g1
     km = k - g1
@@ -103,7 +99,6 @@
     dd = km + kp * q2
     r = g2 - g2 * q2
     t2 = (k + k) * q
-    below = direct * share
     scattered = w * (direct - below)
     rising = scattered * back
     falling = scattered - rising
@@ -115,37 +110,51 @@
     return t, s, (below, new_b, new_q)
 
 
-def descend(cb, gas_ref, big_ref, cos_ref, solar, state_ref, end_ref):
+def product(block, part, turn, gas_ref, big_ref, mix_ref):
+    feats = gas_ref.shape[0]
+    half = big_ref.shape[1] // feats
+    rows = mix_ref.shape[1]
+    cols = pl.ds(pl.multiple_of(block * CB, CB), CB)
+    inputs = gas_ref[:, pl.ds(pl.multiple_of(part * half, half), half), cols].reshape(feats * half, CB)
+    weight = big_ref[turn * rows : (turn + 1) * rows, :]
+    mix_ref[turn] = jnp.dot(weight, inputs, preferred_element_type=jnp.float32)
+
+
+def descend(cb, after, gas_ref, big_ref, cos_ref, solar, mix_ref, state_ref, end_ref):
     feats, lev = gas_ref.shape[0], gas_ref.shape[1]
     gpoints = solar.shape[0]
     rows = 2 * gpoints
     half = big_ref.shape[1] // feats
-    cols = pl.ds(pl.multiple_of(cb * CB, CB), CB)
     mu = cos_ref[pl.ds(cb, 1), :]
-    rate = jnp.broadcast_to(-TAU_SCALE / mu, (gpoints, CB))
+    rate = jnp.broadcast_to((-TAU_SCALE * LOG2E) / mu, (gpoints, CB))
     back = jnp.broadcast_to(0.5 * (1.0 - ASYM * mu), (gpoints, CB))
     top = solar * mu
     zero = jnp.zeros((gpoints, CB), jnp.float32)
     carry = (top, zero, zero)
 
-    for part in range(lev // half):
-        inputs = gas_ref[:, part * half : (part + 1) * half, cols].reshape(feats * half, CB)
-
-        def down(step, carry, part=part, inputs=inputs):
-            at = pl.multiple_of(step * (CHUNK * rows), CHUNK * rows)
-            mix = jnp.dot(
-                big_ref[pl.ds(at, CHUNK * rows), :], inputs, preferred_element_type=jnp.float32
-            )
+    turns = half // CHUNK
+
+    def mixed(block, part, turn):
+        product(block, part, turn, gas_ref, big_ref, mix_ref)
+
+    def down(part, carry):
+        for turn in range(turns):
+            if turn + 1 < turns:
+                mixed(cb, part, turn + 1)
             for i in range(CHUNK):
-                level = part * half + step * CHUNK + i
+                level = part * half + turn * CHUNK + i
                 state_ref[2, level] = carry[1]
                 state_ref[3, level] = carry[2] + carry[0]
-                t, s, carry = layer(mix[i * rows : (i + 1) * rows], gpoints, rate, back, carry)
+                mix = mix_ref[turn, i * rows : (i + 1) * rows, :]
+                t, s, carry = layer(mix, gpoints, rate, back, carry)
                 state_ref[0, level] = t
                 state_ref[1, level] = s
-            return carry
-
-        carry = lax.fori_loop(0, half // CHUNK, down, carry)
+            if turn == turns - 2:
+                last = part == lev // half - 1
+                mixed(jnp.where(last, after, cb), jnp.where(last, 0, part + 1), 0)
+        return carry
+
+    carry = lax.fori_loop(0, lev // half, down, carry)
     for i in range(3):
         end_ref[i] = carry[i]
 
@@ -186,9 +195,9 @@
 
 
 def flux_kernel(
-    n, span, gas_ref, cos_ref, lit_ref, weight_ref, solar_ref, area_ref, fine_albedo_ref, parent_ref,
+    n, span, gas_hbm, cos_ref, lit_ref, weight_ref, solar_ref, area_ref, fine_albedo_ref, parent_ref,
     flux_ref, big_ref, state_ref, end_ref, albedo_ref, cosf_ref, litf_ref, mine_ref, pieces_ref,
-    edge_ref, halo_ref, send_sem, recv_sem, edge_send, edge_recv,
+    edge_ref, halo_ref, mix_ref, gas_ref, send_sem, recv_sem, edge_send, edge_recv, gas_sem,
 ):
     ncb = cos_ref.shape[0]
     blocks = area_ref.shape[0]
@@ -196,6 +205,8 @@
     peers = [lax.rem(me + shift, n) for shift in range(1, n)]
     mesh_id = pl.DeviceIdType.MESH
 
+    load = pltpu.make_async_copy(gas_hbm, gas_ref, gas_sem)
+    load.start()
     barrier = pltpu.get_barrier_semaphore()
     for peer in peers:
         pl.semaphore_signal(barrier, inc=1, device_id={"blk": peer}, device_id_type=mesh_id)
@@ -210,6 +221,26 @@
     litf_ref[...] = lit_ref[...].astype(jnp.float32)
     solar = solar_column(solar_ref)
 
+    def order(i):
+        return jnp.where(i < 2, i * (ncb - 1), i - 1)
+
+    def down(i, slot):
+        after = order(jnp.minimum(i + 1, ncb - 1))
+        descend(
+            order(i), after, gas_ref, big_ref, cosf_ref, solar, mix_ref, state_ref.at[slot], end_ref.at[slot]
+        )
+
+    def up(i, slot, target_ref):
+        ascend(order(i), albedo_ref, litf_ref, state_ref.at[slot], end_ref.at[slot], target_ref)
+
+    load.wait()
+    product(0, 0, 0, gas_ref, big_ref, mix_ref)
+
+    def early_down(i, unused):
+        down(i, i)
+        return unused
+
+    lax.fori_loop(0, 1, early_down, 0)
     pl.semaphore_wait(barrier, n - 1)
     sends = []
     for i, peer in enumerate(peers):
@@ -224,11 +255,8 @@
         copy.start()
         sends.append(copy)
 
-    def edge_down(i, unused):
-        descend(i * (ncb - 1), gas_ref, big_ref, cosf_ref, solar, state_ref.at[i], end_ref.at[i])
-        return unused
-
-    lax.fori_loop(0, 2, edge_down, 0)
+    ahead = state_ref.shape[0]
+    lax.fori_loop(1, ahead, early_down, 0)
     for copy in sends:
         copy.wait()
     start_span = me * (ncb * CB // span)
@@ -238,7 +266,7 @@
     albedo_ref[1] = diffuse
 
     def edge_up(i, unused):
-        ascend(i * (ncb - 1), albedo_ref, litf_ref, state_ref.at[i], end_ref.at[i], edge_ref.at[i])
+        up(i, i, edge_ref.at[i])
         return unused
 
     lax.fori_loop(0, 2, edge_up, 0)
@@ -257,13 +285,21 @@
     flux_ref[:, CB : 2 * CB] = edge_ref[0]
     flux_ref[:, ncb * CB : (ncb + 1) * CB] = edge_ref[1]
 
-    def one(cb, unused):
-        own = pl.ds(pl.multiple_of((cb + 1) * CB, CB), CB)
-        descend(cb, gas_ref, big_ref, cosf_ref, solar, state_ref.at[0], end_ref.at[0])
-        ascend(cb, albedo_ref, litf_ref, state_ref.at[0], end_ref.at[0], flux_ref.at[:, own])
+    def own(i):
+        return flux_ref.at[:, pl.ds(pl.multiple_of((order(i) + 1) * CB, CB), CB)]
+
+    def early_up(i, unused):
+        up(i, i, own(i))
         return unused
 
-    lax.fori_loop(1, ncb - 1, one, 0)
+    lax.fori_loop(2, ahead, early_up, 0)
+
+    def one(i, unused):
+        down(i, 0)
+        up(i, 0, own(i))
+        return unused
+
+    lax.fori_loop(ahead, ncb, one, 0)
     for copy in sends:
         copy.wait()
     flux_ref[:, 0:CB] = halo_ref[1]
@@ -316,12 +352,12 @@
     padded = pl.pallas_call(
         functools.partial(flux_kernel, n, span),
         out_shape=jax.ShapeDtypeStruct((rows, cols + 2 * CB), jnp.float32),
-        in_specs=[full] * 8,
+        in_specs=[pl.BlockSpec(memory_space=pl.ANY)] + [full] * 7,
         out_specs=full,
         scratch_shapes=[
             VMEM((half * 2 * gpoints, half * feats), jnp.bfloat16),
-            VMEM((2, 4, lev, gpoints, CB), jnp.float32),
-            VMEM((2, 3, gpoints, CB), jnp.float32),
+            VMEM((4, 4, lev, gpoints, CB), jnp.float32),
+            VMEM((4, 3, gpoints, CB), jnp.float32),
             VMEM((2, ncb, CB), jnp.float32),
             VMEM((ncb, CB), jnp.float32),
             VMEM((ncb, CB), jnp.float32),
@@ -329,10 +365,13 @@
             VMEM((n - 1, span + 8, 128), jnp.float32),
             VMEM((2, rows, CB), jnp.float32),
             VMEM((2, rows, CB), jnp.float32),
+            VMEM((half // CHUNK, CHUNK * 2 * gpoints, CB), jnp.float32),
+            VMEM((feats, lev, cols), gas_state.dtype),
             pltpu.SemaphoreType.DMA((n - 1,)),
             pltpu.SemaphoreType.DMA((n - 1,)),
             pltpu.SemaphoreType.DMA((2,)),
             pltpu.SemaphoreType.DMA((2,)),
+            pltpu.SemaphoreType.DMA,
         ],
         compiler_params=pltpu.CompilerParams(collective_id=0, has_side_effects=True),
     )(

time: 25.2 us -> 19.5 us (0.77)
  Pallas kernels: 25.1 us -> 19.3 us
    pallas_call x1, Pallas kernels: 22.3 us -> 16.4 us  [local(): pl.pallas_call(functools.partial(flux_kernel, n, span), out_shape=jax.Sha...]
where the time goes in v2:
time: 19.5 us; the launch traced here: 19.3 us
  Pallas kernels  19.3 us (99%)
    pallas_call x1, Pallas kernels, local(): pl.pallas_call(functools.partial(flux_kernel, n, span), out_shape=jax.Sha...  16.4 us
    pallas_call x1, Pallas kernels, local(): pl.pallas_call(side_kernel, out_shape=jax.ShapeDtypeStruct((lev + 1, 2, c...  2.82 us

profile of v2, /device:TPU:0, one launch (start us, length us, event | category | flops | bytes accessed | tf_op | source)
XLA Modules:
  0.0 19.3 jit_solution(6697973221055927666)
XLA Ops:
  0.0 16.4 %shard_map.100.padded_ref = f32[72,1280]{1,0:T(8,128)} custom-call(bf16[16,32,1024]{2,1,0:T(8,128)(2,1)} %gas_hbm.1, bf16[8,128]{1,0:T(8,128)(2,1)} %bitcast.11, s32[8,128]{1,0:T(8,128)} %bitcast.9, bf16[16,64]{1,0:T(8,128)(2,1)} %bitcast.10, f32[1,32]{1,0:T(1,128)} %bitcast.12, f32[32,128]{1,0:T(8,128)} %bitcast.7, f32[2,4096]{1,0:T(2,128)} %fine_albedo_ref.1, ...), custom_call_target="tpu_custom_call" | custom-call | tf_op jit(solution)/shard_map/pallas_call | solution.py:352
  16.4 2.8 %shard_map.101 = f32[33,2,1024]{2,1,0:T(2,128)} custom-call(f32[72,1280]{1,0:T(8,128)} %shard_map.100.padded_ref, s32[3,1024]{1,0:T(4,128)} %neighbours_ref.1, f32[3,1024]{1,0:T(4,128)} %weights_ref.1), custom_call_target="tpu_custom_call" | custom-call | tf_op jit(solution)/shard_map/pallas_call | solution.py:382
